TPU v7x, 32 devices: a whole 2x2x4 slice. The times are simulated.
32 devices in a mesh: dp: 8 (over z, y), head: 4 (over x, core).
Axes of the slice: x: 2, y: 2, z: 4, core: 2. Of those that a mesh axis runs over, the one named last changes fastest.
Arguments:
- tokens: bfloat16 [32768, 768], P(('dp', 'head')), may hold values from -6 to 6
- seq_lengths: int32 [64, 32], P('dp'), may hold values from 0 to 512, as said below
- qkv_weight: bfloat16 [2, 3, 768, 768], P(None, None, None, 'head'), may hold values from -0.21875 to 0.21875
- qv_bias: float32 [2, 2, 768], P(None, None, 'head'), may hold values from -3 to 3
- out_weight: bfloat16 [2, 768, 768], replicated, may hold values from -0.875 to 0.875
- out_bias: float32 [2, 768], replicated, may hold values from -3 to 3
- norm1_gain: float32 [2, 768], replicated, may hold values from 0.25 to 1.75
- norm1_shift: float32 [2, 768], replicated, may hold values from -3 to 3
- up_weight: bfloat16 [2, 768, 3072], replicated, may hold values from -0.21875 to 0.21875
- up_bias: float32 [2, 3072], replicated, may hold values from -3 to 3
- down_weight: bfloat16 [2, 3072, 768], replicated, may hold values from -0.109375 to 0.109375
- down_bias: float32 [2, 768], replicated, may hold values from -3 to 3
- norm2_gain: float32 [2, 768], replicated, may hold values from 0.25 to 1.75
- norm2_shift: float32 [2, 768], replicated, may hold values from -3 to 3
- out_grad: bfloat16 [32768, 768], P(('dp', 'head')), may hold values from -6 to 6
Outputs:
- out_state: bfloat16 [32768, 768], P(('dp', 'head'))
- input_grad: bfloat16 [32768, 768], P(('dp', 'head'))
- qkv_weight_grad: float32 [2, 3, 768, 768], P(None, None, 'dp', 'head')
- qv_bias_grad: float32 [2, 2, 768], replicated
- out_weight_grad: float32 [2, 768, 768], P(None, 'dp', 'head')
- out_bias_grad: float32 [2, 768], replicated
- norm1_gain_grad: float32 [2, 768], replicated
- norm1_shift_grad: float32 [2, 768], replicated
- up_weight_grad: float32 [2, 768, 3072], P(None, 'dp', 'head')
- up_bias_grad: float32 [2, 3072], replicated
- down_weight_grad: float32 [2, 3072, 768], P(None, 'head', 'dp')
- down_bias_grad: float32 [2, 768], replicated
- norm2_gain_grad: float32 [2, 768], replicated
- norm2_shift_grad: float32 [2, 768], replicated
Inputs may be any that keep to these rules, and one draw needn't show every extreme that they name: `seq_lengths`: each slot's row sums to 512; nonzero entries come first and zero entries mark no sequence; some slot holds a single sequence of 512 rows.
All inputs are finite; a program needn't handle non-finite values.
Results may differ from a plain program's by a relative error of at most 0.025.
Values may be sent and summed in bfloat16 or wider, within the bound.
No kernel may reach another device: no remote copies, remote signals or barrier semaphores. Data moves between devices by JAX's collectives and lax.ppermute only.
A program may use at most 256 MiB of HBM per device.

v0:
```python
import jax
import jax.numpy as jnp
from jax import lax
from jax.sharding import PartitionSpec as P

HD = 64
EPSILON = 1e-06


def norm_rows(values, gain, shift):
    centre = jnp.mean(values, axis=-1, keepdims=True)
    centred = values - centre
    spread = jnp.mean(centred * centred, axis=-1, keepdims=True)
    return centred * lax.rsqrt(spread + EPSILON) * gain + shift


def exact_gelu(values):
    return jax.nn.gelu(values, approximate=False)


def segment_ids(lengths, slot_rows):
    boundary = jnp.cumsum(lengths, axis=1)
    position = jnp.arange(slot_rows, dtype=jnp.int32)
    return jnp.sum((position[None, :, None] >= boundary[:, None, :]).astype(jnp.int32), axis=2)


def slot_scores(queries, keys_in, segments):
    scaling = queries.shape[-1] ** (-0.5)
    scores = (
        jnp.einsum("qhd,khd->hqk", queries, keys_in, preferred_element_type=jnp.float32) * scaling
    )
    inside = (segments[:, None] == segments[None, :])[None]
    return (scores, inside)


def slot_forward(packed):
    queries, keys_in, values_in, segments = packed
    scores, inside = slot_scores(queries, keys_in, segments)
    scores = jnp.where(inside, scores, -1e30)
    peak_score = jnp.max(scores, axis=-1, keepdims=True)
    weights = jnp.exp(scores - peak_score)
    denominator = jnp.sum(weights, axis=-1, keepdims=True)
    probability = (weights / denominator).astype(jnp.bfloat16)
    context = jnp.einsum("hqk,khd->qhd", probability, values_in, preferred_element_type=jnp.float32)
    return (context.astype(jnp.bfloat16), (peak_score + jnp.log(denominator))[..., 0])


def slot_backward(packed):
    queries, keys_in, values_in, grad_context, log_total, segments = packed
    scaling = queries.shape[-1] ** (-0.5)
    scores, inside = slot_scores(queries, keys_in, segments)
    probability = jnp.where(inside, jnp.exp(scores - log_total[..., None]), 0.0)
    grad_prob = jnp.einsum(
        "qhd,khd->hqk", grad_context, values_in, preferred_element_type=jnp.float32
    )
    shares = jnp.sum(probability * grad_prob, axis=-1, keepdims=True)
    grad_score = (probability * (grad_prob - shares)).astype(jnp.bfloat16)
    grad_query = (
        jnp.einsum("hqk,khd->qhd", grad_score, keys_in, preferred_element_type=jnp.float32)
        * scaling
    )
    grad_key = (
        jnp.einsum("hqk,qhd->khd", grad_score, queries, preferred_element_type=jnp.float32)
        * scaling
    )
    grad_value = jnp.einsum(
        "hqk,qhd->khd",
        probability.astype(jnp.bfloat16),
        grad_context,
        preferred_element_type=jnp.float32,
    )
    return (
        grad_query.astype(jnp.bfloat16),
        grad_key.astype(jnp.bfloat16),
        grad_value.astype(jnp.bfloat16),
    )


def on_device(
    tokens,
    seq_lengths,
    qkv_weight,
    qv_bias,
    out_weight,
    out_bias,
    norm1_gain,
    norm1_shift,
    up_weight,
    up_bias,
    down_weight,
    down_bias,
    norm2_gain,
    norm2_shift,
    out_grad,
):
    heads_count = lax.axis_size("head")
    head_index = lax.axis_index("head")
    local_rows, model_width = tokens.shape
    group_rows = local_rows * heads_count
    slots_here = seq_lengths.shape[0]
    slot_rows = group_rows // slots_here
    segments = segment_ids(seq_lengths, slot_rows)
    head_width = qkv_weight.shape[-1]
    local_heads = head_width // HD
    layers = qkv_weight.shape[0]
    qkv_shape = (slots_here, slot_rows, 3, local_heads, HD)
    hidden_state = tokens.astype(jnp.float32)
    kept_values = []
    for layer_index in range(layers):
        gathered = lax.all_gather(hidden_state.astype(jnp.bfloat16), "head", axis=0, tiled=True)
        projected = jnp.einsum(
            "rd,cde->rce", gathered, qkv_weight[layer_index], preferred_element_type=jnp.float32
        )
        bias_rows = jnp.stack(
            [
                qv_bias[layer_index, 0],
                jnp.zeros_like(qv_bias[layer_index, 0]),
                qv_bias[layer_index, 1],
            ]
        )
        projected = (projected + bias_rows[None]).astype(jnp.bfloat16)
        shaped = projected.reshape(qkv_shape)
        context, log_total = lax.map(
            slot_forward, (shaped[:, :, 0], shaped[:, :, 1], shaped[:, :, 2], segments)
        )
        context = context.reshape(group_rows, head_width)
        token_context = lax.all_to_all(context, "head", split_axis=0, concat_axis=1, tiled=True)
        attended = (
            jnp.dot(token_context, out_weight[layer_index], preferred_element_type=jnp.float32)
            + out_bias[layer_index]
        )
        first_sum = hidden_state + attended
        normed = norm_rows(first_sum, norm1_gain[layer_index], norm1_shift[layer_index])
        normed_low = normed.astype(jnp.bfloat16)
        ffn_rows = normed_low
        up_part = up_weight[layer_index]
        up_shift = up_bias[layer_index]
        down_part = down_weight[layer_index]
        before_gelu = jnp.dot(ffn_rows, up_part, preferred_element_type=jnp.float32) + up_shift
        activated = exact_gelu(before_gelu).astype(jnp.bfloat16)
        branch = jnp.dot(activated, down_part, preferred_element_type=jnp.float32)
        second_sum = normed + branch + down_bias[layer_index]
        hidden_state = norm_rows(second_sum, norm2_gain[layer_index], norm2_shift[layer_index])
        kept_values.append(
            (
                gathered,
                projected,
                log_total,
                token_context,
                first_sum,
                ffn_rows,
                up_part,
                down_part,
                before_gelu,
                activated,
                second_sum,
            )
        )
    out_state = hidden_state.astype(jnp.bfloat16)
    grad_state = out_grad.astype(jnp.float32)
    ffn_list, proj_list, attn_list, small_list, shift_list = ([], [], [], [], [])
    for layer_index in reversed(range(layers)):
        (
            gathered,
            projected,
            log_total,
            token_context,
            first_sum,
            ffn_rows,
            up_part,
            down_part,
            before_gelu,
            activated,
            second_sum,
        ) = kept_values[layer_index]
        pull_second = jax.vjp(
            norm_rows, second_sum, norm2_gain[layer_index], norm2_shift[layer_index]
        )[1]
        grad_second, grad_gain2, grad_shift2 = pull_second(grad_state)
        grad_branch = grad_second.astype(jnp.bfloat16)
        grad_down_shift = jnp.sum(grad_branch.astype(jnp.float32), axis=0)
        grad_down = jnp.einsum(
            "rd,rf->df", grad_branch, activated, preferred_element_type=jnp.float32
        )
        grad_act = jnp.einsum(
            "rd,fd->rf", grad_branch, down_part, preferred_element_type=jnp.float32
        )
        pull_gelu = jax.vjp(exact_gelu, before_gelu)[1]
        grad_pre = pull_gelu(grad_act)[0].astype(jnp.bfloat16)
        grad_up_shift = jnp.sum(grad_pre.astype(jnp.float32), axis=0)
        grad_up = jnp.einsum("rd,rf->df", ffn_rows, grad_pre, preferred_element_type=jnp.float32)
        grad_normed_low = jnp.einsum(
            "rf,df->rd", grad_pre, up_part, preferred_element_type=jnp.float32
        )
        grad_normed = grad_second + grad_normed_low
        pull_first = jax.vjp(
            norm_rows, first_sum, norm1_gain[layer_index], norm1_shift[layer_index]
        )[1]
        grad_first, grad_gain1, grad_shift1 = pull_first(grad_normed)
        grad_attended = grad_first.astype(jnp.bfloat16)
        grad_out_shift = jnp.sum(grad_attended.astype(jnp.float32), axis=0)
        grad_out = jnp.einsum(
            "rd,re->de", token_context, grad_attended, preferred_element_type=jnp.float32
        )
        grad_mixed = jnp.einsum(
            "re,de->rd", grad_attended, out_weight[layer_index], preferred_element_type=jnp.float32
        ).astype(jnp.bfloat16)
        grad_context = lax.all_to_all(grad_mixed, "head", split_axis=1, concat_axis=0, tiled=True)
        shaped = projected.reshape(qkv_shape)
        grad_query, grad_key, grad_value = lax.map(
            slot_backward,
            (
                shaped[:, :, 0],
                shaped[:, :, 1],
                shaped[:, :, 2],
                grad_context.reshape(slots_here, slot_rows, local_heads, HD),
                log_total,
                segments,
            ),
        )
        grad_proj = jnp.stack([grad_query, grad_key, grad_value], axis=2).reshape(
            group_rows, 3, head_width
        )
        grad_qkv = jnp.einsum(
            "rd,rce->cde", gathered, grad_proj, preferred_element_type=jnp.float32
        )
        bias_local = jnp.sum(grad_proj.astype(jnp.float32), axis=0)
        qv_local = jnp.stack([bias_local[0], bias_local[2]])
        qv_full = lax.dynamic_update_slice_in_dim(
            jnp.zeros((2, model_width), jnp.float32), qv_local, head_index * head_width, 1
        )
        layer_weights = qkv_weight[layer_index]
        grad_state = grad_first + lax.psum_scatter(
            jnp.einsum(
                "rce,cde->rd", grad_proj, layer_weights, preferred_element_type=jnp.float32
            ).astype(jnp.bfloat16),
            "head",
            scatter_dimension=0,
            tiled=True,
        ).astype(jnp.float32)
        ffn_list.append(jnp.stack([grad_up, grad_down]))
        proj_list.append(grad_out)
        attn_list.append(grad_qkv)
        small_list.append(
            jnp.concatenate(
                [
                    qv_full,
                    jnp.stack(
                        [
                            grad_out_shift,
                            grad_gain1,
                            grad_shift1,
                            grad_down_shift,
                            grad_gain2,
                            grad_shift2,
                        ]
                    ),
                ],
                axis=0,
            )
        )
        shift_list.append(grad_up_shift)
    input_grad = grad_state.astype(jnp.bfloat16)
    ffn_stack = jnp.stack(ffn_list[::-1])
    proj_stack = jnp.stack(proj_list[::-1])
    attn_stack = jnp.stack(attn_list[::-1])
    small_stack = jnp.stack(small_list[::-1])
    shift_stack = jnp.stack(shift_list[::-1])
    ffn_data, proj_data, attn_data = (
        lax.psum_scatter(
            ffn_stack.astype(jnp.bfloat16), "dp", scatter_dimension=2, tiled=True
        ).astype(jnp.float32),
        lax.psum_scatter(
            proj_stack.astype(jnp.bfloat16), "dp", scatter_dimension=1, tiled=True
        ).astype(jnp.float32),
        lax.psum_scatter(
            attn_stack.astype(jnp.bfloat16), "dp", scatter_dimension=2, tiled=True
        ).astype(jnp.float32),
    )
    ffn_head, proj_head = (
        lax.psum_scatter(
            ffn_data.astype(jnp.bfloat16), "head", scatter_dimension=3, tiled=True
        ).astype(jnp.float32),
        lax.psum_scatter(
            proj_data.astype(jnp.bfloat16), "head", scatter_dimension=2, tiled=True
        ).astype(jnp.float32),
    )
    small_sum, shift_sum = lax.psum((small_stack, shift_stack), ("dp", "head"))
    down_weight_grad = jnp.transpose(ffn_head[:, 1], (0, 2, 1))
    return (
        out_state,
        input_grad,
        attn_data,
        small_sum[:, 0:2],
        proj_head,
        small_sum[:, 2],
        small_sum[:, 3],
        small_sum[:, 4],
        ffn_head[:, 0],
        shift_sum,
        down_weight_grad,
        small_sum[:, 5],
        small_sum[:, 6],
        small_sum[:, 7],
    )


def solution(mesh):
    in_specs = (
        P(("dp", "head"), None),
        P("dp", None),
        P(None, None, None, "head"),
        P(None, None, "head"),
        P(),
        P(),
        P(),
        P(),
        P(),
        P(),
        P(),
        P(),
        P(),
        P(),
        P(("dp", "head"), None),
    )
    out_specs = (
        P(("dp", "head"), None),
        P(("dp", "head"), None),
        P(None, None, "dp", "head"),
        P(),
        P(None, "dp", "head"),
        P(),
        P(),
        P(),
        P(None, "dp", "head"),
        P(),
        P(None, "head", "dp"),
        P(),
        P(),
        P(),
    )
    return jax.shard_map(
        on_device, mesh=mesh, in_specs=in_specs, out_specs=out_specs, check_vma=False
    )
```

profile of v0, /device:TPU:0, one launch (start us, length us, event | category | flops | bytes accessed | tf_op | source)
XLA Modules:
  0.0 1406.1 jit_solution(3311266776964060774)
XLA Ops:
  12.9 45.8 %all-gather.3.cloned.1.call-done = bf16[4096,768]{1,0:T(8,128)(2,1)} async-done(((bf16[1024,768]{1,0:T(8,128)(2,1)}), bf16[4096,768]{1,0:T(8,128)(2,1)}) %all-gather.3.cloned.1.call-update) | async-done | bytes 6291472 | tf_op jit(solution)/shard_map/all_gather | solution.py:110
  73.9 35.4 %while.52 = (s32[]{:T(128)}, bf16[8,512,3,64]{1,3,2,0:T(8,128)(2,1)}, f32[8,3,512]{2,1,0:T(4,128)S(1)}, bf16[8,512,3,64]{1,3,2,0:T(8,128)(2,1)}, s32[8,512]{1,0:...) while((s32[]{:T(128)}, ...), condition=%wide.region_5.6_spmd, body=%wide.region_2.5_spmd.sunk | while | flops 211122688 | bytes 11335773 | solution.py:123
  113.8 13.7 all_to_all.52
  139.1 15.2 %all-to-all-done = bf16[4,1024,192]{1,2,0:T(8,128)(2,1)S(1)} async-done(((bf16[4,1024,192]{1,2,0:T(8,128)(2,1)}), bf16[4,1024,192]{1,2,0:T(8,128)(2,1)S(1)}, u32[]{:S(2)}, u32[]{:S(2)}) %all-to-all-start) | async-done | bytes 1572896 | tf_op jit(solution)/shard_map/all_to_all | solution.py:127
  158.9 38.8 %multiply_convert_fusion.3 = (bf16[1024,3072]{1,0:T(8,128)(2,1)}, f32[1024,3072]{1,0:T(8,128)}, f32[1024,3072]{1,0:T(8,128)}) fusion(f32[3072]{0:T(1024)S(1)} %bitcast.494, bf16[2,768,3072]{2,1,0:T(8,128)(2,1)} %param.31, f32[1024,768]{0,1:T(8,128)S(1)} %get-tuple-element.478, f32[768]{0:T(1024)S(1)} %get-tuple-element.347, ...), kind=kOutput, calls=%fused_computation.148 | convolution fusion | flops 5043388416 | bytes 39348224 | tf_op jit(solution)/shard_map/dot_general | solution.py:139
  208.6 46.5 %all-gather.5.cloned.1.call-done = bf16[4096,768]{0,1:T(8,128)(2,1)} async-done(((bf16[1024,768]{0,1:T(8,128)(2,1)}), bf16[4096,768]{0,1:T(8,128)(2,1)}) %all-gather.5.cloned.1.call-update) | async-done | bytes 6291472 | tf_op jit(solution)/shard_map/all_gather | solution.py:110
  273.1 43.5 %while.53 = (s32[]{:T(128)}, bf16[8,512,3,64]{1,3,2,0:T(8,128)(2,1)}, f32[8,3,512]{2,1,0:T(4,128)S(1)}, bf16[8,512,3,64]{1,3,2,0:T(8,128)(2,1)}, s32[8,512]{1,0:...) while((s32[]{:T(128)}, ...), condition=%wide.region_13.14_spmd, body=%wide.region_10.13_spmd.sunk | while | flops 211122688 | bytes 11335773 | solution.py:123
  334.3 17.5 %all-to-all-done.1 = bf16[4,1024,192]{1,2,0:T(8,128)(2,1)} async-done(((bf16[4,1024,192]{1,2,0:T(8,128)(2,1)}), bf16[4,1024,192]{1,2,0:T(8,128)(2,1)}, u32[]{:S(2)}, u32[]{:S(2)}) %all-to-all-start.1) | async-done | bytes 1572896 | tf_op jit(solution)/shard_map/all_to_all | solution.py:127
  356.5 38.4 %multiply_convert_fusion.2 = (bf16[1024,3072]{1,0:T(8,128)(2,1)}, f32[1024,3072]{1,0:T(8,128)}, f32[1024,3072]{1,0:T(8,128)}) fusion(f32[3072]{0:T(1024)S(1)} %bitcast.497, bf16[2,768,3072]{2,1,0:T(8,128)(2,1)} %param.31, f32[1024,768]{0,1:T(8,128)S(1)} %get-tuple-element.483, f32[768]{0:T(1024)S(1)} %copy-done.73, f32[768]{0:T(1024)S(1)} %copy-done.52, ...), kind=kOutput, calls=%fused_computation.135 | convolution fusion | flops 5043388416 | bytes 39348224 | tf_op jit(solution)/shard_map/dot_general | solution.py:139
  411.1 18.2 %convert_reduce_fusion = (f32[3072]{0:T(1024)}, bf16[1024,3072]{1,0:T(8,128)(2,1)}) fusion(f32[1024,3072]{1,0:T(8,128)} %get-tuple-element.435, bf16[1024,768]{0,1:T(8,128)(2,1)S(1)} %get-tuple-element.425, bf16[2,3072,768]{2,1,0:T(8,128)(2,1)} %param.33, f32[1024,3072]{1,0:T(8,128)} %get-tuple-element.484, f32[3072]{0:T(1024)S(1)} %bitcast.498), kind=kOutput, calls=%fused_computation.131 | convolution fusion | flops 4885312512 | bytes 37773312 | tf_op jit(solution)/shard_map/rd,fd->rf/dot_general | solution.py:185
  429.4 11.7 multiply_reduce_fusion.2
  451.5 20.0 %all-to-all-done.2 = bf16[1024,4,192]{0,2,1:T(8,128)(2,1)S(1)} async-done(((bf16[1024,4,192]{0,2,1:T(8,128)(2,1)}), bf16[1024,4,192]{0,2,1:T(8,128)(2,1)S(1)}, u32[]{:S(2)}, u32[]{:S(2)}) %all-to-all-start.2) | async-done | bytes 1572896 | tf_op jit(solution)/shard_map/all_to_all | solution.py:208
  479.6 88.1 %while.54 = (s32[]{:T(128)}, bf16[8,512,3,64]{1,3,2,0:T(8,128)(2,1)S(1)}, bf16[8,512,3,64]{1,3,2,0:T(8,128)(2,1)}, bf16[8,512,3,64]{1,3,2,0:T(8,128)(2,1)}, bf16...) while((s32[]{:T(128)}, ...), condition=%wide.region_24.25_spmd, body=%wide.region_22.24_spmd.sunk | while | flops 511146496 | bytes 26125428 | solution.py:210
  598.8 11.7 fusion.140
  610.5 41.4 %reduce-scatter.12.cloned.1.call-done = bf16[1024,768]{0,1:T(8,128)(2,1)} async-done(((bf16[4096,768]{0,1:T(8,128)(2,1)}), bf16[1024,768]{0,1:T(8,128)(2,1)}) %reduce-scatter.12.cloned.1.call-update) | async-done | bytes 1572880 | tf_op jit(solution)/shard_map/reduce_scatter | solution.py:233
  659.1 18.5 %convert_reduce_fusion.1 = (f32[3072]{0:T(1024)S(1)}, bf16[1024,3072]{1,0:T(8,128)(2,1)}) fusion(f32[1024,3072]{1,0:T(8,128)} %get-tuple-element.437, bf16[1024,768]{0,1:T(8,128)(2,1)} %get-tuple-element.421, bf16[2,3072,768]{2,1,0:T(8,128)(2,1)} %param.33, f32[1024,3072]{1,0:T(8,128)} %get-tuple-element.479, f32[3072]{0:T(1024)S(1)} %bitcast.495), kind=kOutput, calls=%fused_computation.132 | convolution fusion | flops 4885312512 | bytes 37773312 | tf_op jit(solution)/shard_map/rd,fd->rf/dot_general | solution.py:185
  738.1 16.7 %pad_maximum_fusion = bf16[2,2,768,3072]{3,2,1,0:T(8,128)(2,1)} fusion(bf16[1,2,768,3072]{3,2,1,0:T(8,128)(2,1)} %maximum_bitcast_fusion.1, bf16[1,2,768,3072]{3,2,1,0:T(8,128)(2,1)} %maximum_bitcast_fusion), kind=kLoop, calls=%fused_computation.126 | loop fusion | flops 9437184 | bytes 37748736 | tf_op jit(solution)/shard_map/stack | solution.py:264
  802.2 101.9 %while.55 = (s32[]{:T(128)}, bf16[8,512,3,64]{1,3,2,0:T(8,128)(2,1)}, bf16[8,512,3,64]{1,3,2,0:T(8,128)(2,1)}, bf16[8,512,3,64]{1,3,2,0:T(8,128)(2,1)}, bf16[8,5...) while((s32[]{:T(128)}, ...), condition=%wide.region_32.33_spmd, body=%wide.region_30.32_spmd.sunk | while | flops 511146496 | bytes 26125428 | solution.py:210
  966.8 112.1 %reduce-scatter.18.cloned.1.call-done = bf16[2,2,96,3072]{3,2,1,0:T(8,128)(2,1)} async-done(((bf16[2,2,768,3072]{3,2,1,0:T(8,128)(2,1)}), bf16[2,2,96,3072]{3,2,1,0:T(8,128)(2,1)}) %reduce-scatter.18.cloned.1.call-update) | async-done | bytes 2359312 | tf_op jit(solution)/shard_map/reduce_scatter | solution.py:270
  1081.6 122.8 %all-reduce.3.cloned.1.call-done = (f32[2,8,768]{2,0,1:T(2,128)}, f32[2,3072]{1,0:T(2,128)}) async-done(((f32[2,8,768]{2,0,1:T(2,128)}, f32[2,3072]{1,0:T(2,128)}), (f32[2,8,768]{2,0,1:T(2,128)}, f32[2,3072]{1,0:T(2,128)})) %all-reduce.3.cloned.1.call-update) | async-done | bytes 73744 | tf_op jit(solution)/shard_map/psum | solution.py:288
  1207.1 69.8 %reduce-scatter.22.cloned.1.call-done = bf16[96,1152]{1,0:T(8,128)(2,1)} async-done(((bf16[768,1152]{1,0:T(8,128)(2,1)}), bf16[96,1152]{1,0:T(8,128)(2,1)}) %reduce-scatter.22.cloned.1.call-update) | async-done | bytes 221200
  1281.1 18.6 %reduce-scatter.24.cloned.1.call-done = bf16[192,192]{1,0:T(8,128)(2,1)} async-done(((bf16[768,192]{1,0:T(8,128)(2,1)}), bf16[192,192]{1,0:T(8,128)(2,1)}) %reduce-scatter.24.cloned.1.call-update) | async-done | bytes 73744
  1301.4 59.1 %reduce-scatter.14.cloned.1.call-done = bf16[1024,768]{0,1:T(8,128)(2,1)} async-done(((bf16[4096,768]{0,1:T(8,128)(2,1)}), bf16[1024,768]{0,1:T(8,128)(2,1)}) %reduce-scatter.14.cloned.1.call-update) | async-done | bytes 1572880 | tf_op jit(solution)/shard_map/reduce_scatter | solution.py:233
  1366.3 29.9 %reduce-scatter.20.cloned.1.call-done = bf16[2,2,96,768]{3,2,1,0:T(8,128)(2,1)} async-done(((bf16[2,2,96,3072]{3,2,1,0:T(8,128)(2,1)}), bf16[2,2,96,768]{3,2,1,0:T(8,128)(2,1)}) %reduce-scatter.20.cloned.1.call-update) | async-done | bytes 589840 | tf_op jit(solution)/shard_map/reduce_scatter | solution.py:281
  (599 shorter events, 623.1 us)
Async XLA Ops:
  7.2 51.5 %all-gather.3.cloned.1.call-start = ((), (), s32[]{:S(2)}) async-start(), calls=%async_computation.11 | async-start | bytes 7864320 | tf_op jit(solution)/shard_map/all_gather | solution.py:110
  130.6 23.8 %all-to-all-start = ((bf16[4,1024,192]{1,2,0:T(8,128)(2,1)}), bf16[4,1024,192]{1,2,0:T(8,128)(2,1)S(1)}, u32[]{:S(2)}, u32[]{:S(2)}) async-start(bf16[4,1024,192]{1,2,0:T(8,128)(2,1)} %copy.160), calls=%async_computation | async-start | bytes 3145728 | tf_op jit(solution)/shard_map/all_to_all | solution.py:127
  134.3 120.8 %all-gather.5.cloned.1.call-start = ((), (), s32[]{:S(2)}) async-start(), calls=%async_computation.12 | async-start | bytes 7864320 | tf_op jit(solution)/shard_map/all_gather | solution.py:110
  137.9 59.8 %copy-start.50 = (f32[768]{0:T(1024)}, f32[768]{0:T(1024)S(1)}, u32[]{:S(2)}) copy-start(f32[768]{0:T(1024)S(1)} %get-tuple-element.495) | copy-start | bytes 9220
  137.9 59.8 %copy-start.71 = (f32[768]{0:T(1024)}, f32[768]{0:T(1024)S(1)}, u32[]{:S(2)}) copy-start(f32[768]{0:T(1024)S(1)} %get-tuple-element.347) | copy-start | bytes 9220
  138.5 213.3 %copy-start.35 = (f32[768]{0:T(1024)}, f32[768]{0:T(1024)S(1)}, u32[]{:S(2)}) copy-start(f32[768]{0:T(1024)S(1)} %get-tuple-element.497) | copy-start | bytes 9220
  206.4 145.4 %copy-start = (f32[1024,768]{0,1:T(8,128)}, f32[1024,768]{0,1:T(8,128)S(1)}, u32[]{:S(2)}) copy-start(f32[1024,768]{0,1:T(8,128)S(1)} %get-tuple-element.481) | copy-start | bytes 9437188
  206.4 145.4 %copy-start.33 = (f32[1024]{0:T(1024)}, f32[1024]{0:T(1024)S(1)}, u32[]{:S(2)}) copy-start(f32[1024]{0:T(1024)S(1)} %broadcast_multiply_fusion.2) | copy-start | bytes 12292
  206.8 145.0 %copy-start.37 = (f32[1024]{0:T(1024)}, f32[1024]{0:T(1024)S(1)}, u32[]{:S(2)}) copy-start(f32[1024]{0:T(1024)S(1)} %fusion.190) | copy-start | bytes 12292
  327.0 24.8 %all-to-all-start.1 = ((bf16[4,1024,192]{1,2,0:T(8,128)(2,1)}), bf16[4,1024,192]{1,2,0:T(8,128)(2,1)}, u32[]{:S(2)}, u32[]{:S(2)}) async-start(bf16[4,1024,192]{1,2,0:T(8,128)(2,1)} %copy.166), calls=%async_computation.1 | async-start | bytes 3145728 | tf_op jit(solution)/shard_map/all_to_all | solution.py:127
  447.9 23.6 %all-to-all-start.2 = ((bf16[1024,4,192]{0,2,1:T(8,128)(2,1)}), bf16[1024,4,192]{0,2,1:T(8,128)(2,1)S(1)}, u32[]{:S(2)}, u32[]{:S(2)}) async-start(bf16[1024,4,192]{0,2,1:T(8,128)(2,1)} %bitcast.68), calls=%async_computation.2 | async-start | bytes 3145728 | tf_op jit(solution)/shard_map/all_to_all | solution.py:208
  451.4 200.5 %reduce-scatter.12.cloned.1.call-start = ((), (), s32[]{:S(2)}) async-start(), calls=%async_computation.13 | async-start | bytes 7864320 | tf_op jit(solution)/shard_map/reduce_scatter | solution.py:233
  593.4 361.3 %reduce-scatter.16.cloned.1.call-start = ((), (), s32[]{:S(2)}) async-start(), calls=%async_computation.15 | async-start | bytes 2654208 | tf_op jit(solution)/shard_map/reduce_scatter | solution.py:273
  598.8 53.1 %copy-start.1 = (f32[1024,768]{0,1:T(8,128)S(1)}, f32[1024,768]{0,1:T(8,128)}, u32[]{:S(2)}) copy-start(f32[1024,768]{0,1:T(8,128)} %copy-done) | copy-start | bytes 9437188
  598.8 53.1 %copy-start.34 = (f32[1024]{0:T(1024)S(1)}, f32[1024]{0:T(1024)}, u32[]{:S(2)}) copy-start(f32[1024]{0:T(1024)} %copy-done.33) | copy-start | bytes 12292
  598.8 53.1 %copy-start.36 = (f32[768]{0:T(1024)S(1)}, f32[768]{0:T(1024)}, u32[]{:S(2)}) copy-start(f32[768]{0:T(1024)} %copy-done.35) | copy-start | bytes 9220
  598.8 53.1 %copy-start.38 = (f32[1024]{0:T(1024)S(1)}, f32[1024]{0:T(1024)}, u32[]{:S(2)}) copy-start(f32[1024]{0:T(1024)} %copy-done.37) | copy-start | bytes 12292
  693.2 385.8 %reduce-scatter.18.cloned.1.call-start = ((), (), s32[]{:S(2)}) async-start(), calls=%async_computation.16 | async-start | bytes 21233664 | tf_op jit(solution)/shard_map/reduce_scatter | solution.py:270
  763.2 24.5 %all-to-all-start.3 = ((bf16[1024,4,192]{0,2,1:T(8,128)(2,1)}), bf16[1024,4,192]{0,2,1:T(8,128)(2,1)}, u32[]{:S(2)}, u32[]{:S(2)}) async-start(bf16[1024,4,192]{0,2,1:T(8,128)(2,1)} %bitcast.483), calls=%async_computation.4 | async-start | bytes 3145728 | tf_op jit(solution)/shard_map/all_to_all | solution.py:208
  767.6 436.8 %all-reduce.3.cloned.1.call-start = ((), (), s32[]{:S(2)}) async-start(), calls=%async_computation.20 | async-start | bytes 147456 | tf_op jit(solution)/shard_map/psum | solution.py:288
  932.0 344.8 %reduce-scatter.22.cloned.1.call-start = ((), (), s32[]{:S(2)}) async-start(), calls=%async_computation.18 | async-start | bytes 1990656
  954.6 345.0 %reduce-scatter.24.cloned.1.call-start = ((), (), s32[]{:S(2)}) async-start(), calls=%async_computation.19 | async-start | bytes 491520
  957.0 403.6 %reduce-scatter.14.cloned.1.call-start = ((), (), s32[]{:S(2)}) async-start(), calls=%async_computation.14 | async-start | bytes 7864320 | tf_op jit(solution)/shard_map/reduce_scatter | solution.py:233
  966.8 429.4 %reduce-scatter.20.cloned.1.call-start = ((), (), s32[]{:S(2)}) async-start(), calls=%async_computation.17 | async-start | bytes 2949120 | tf_op jit(solution)/shard_map/reduce_scatter | solution.py:281
  (75 other events, 1029.3 us)
Sparse Core Ops, SparseCore 0:
  9.6 49.0 all-gather.2
  208.7 46.3 all-gather.4
  593.5 58.3 reduce-scatter.11
  693.3 69.0 reduce-scatter.15
  766.6 312.3 reduce-scatter.17
  1086.6 117.7 all-reduce.2
  1208.2 68.5 reduce-scatter.21
  1279.9 19.7 reduce-scatter.23
  1302.2 58.3 reduce-scatter.13
  1363.1 33.0 reduce-scatter.19
where the time goes:
time: 1420 us; the launch traced here: 1410 us
  waiting for transfers between devices  610 us (43%)
  matrix products  475 us (33%)
  local copies, waits for them, and re-layouts  185 us (13%)
  other arithmetic  102 us (7%)
  starting transfers between devices  17.2 us (1%)
  between operations  15.7 us (1%)
    psum x1, waiting for transfers between devices, on_device(): small_sum, shift_sum = lax.psum((small_stack, shift_stack), ('dp', 'head'))  123 us
    reduce_scatter x1, waiting for transfers between devices, on_device(): lax.psum_scatter(ffn_stack.astype(jnp.bfloat16), 'dp', scatter_dimension=...  112 us
    reduce_scatter x2, waiting for transfers between devices, on_device(): lax.psum_scatter(jnp.einsum('rce,cde->rd', grad_proj, layer_weights, pref...  101 us
    all_gather x2, waiting for transfers between devices, on_device(): lax.all_gather(hidden_state.astype(jnp.bfloat16), 'head', axis=0, tiled=T...  92.3 us
    unnamed x12, waiting for transfers between devices  89.2 us
    dot_general x2, matrix products, on_device(): jnp.dot(ffn_rows, up_part, preferred_element_type=jnp.float32) + up_shift  77.2 us
    unnamed x195, local copies, waits for them, and re-layouts  57.6 us
    dot_general x32, matrix products, slot_scores(): jnp.einsum('qhd,khd->hqk', queries, keys_in, preferred_element_type=jnp.f...  55.1 us
  transfers between devices with their start and end apart: 14, of which 13 were waited for; matrix products, arithmetic and copies ran while one was open for 21% of the time, Pallas kernels for 0%

commit v1 on v0

--- a/solution.py
+++ b/solution.py
@@ -124,7 +124,10 @@
             slot_forward, (shaped[:, :, 0], shaped[:, :, 1], shaped[:, :, 2], segments)
         )
         context = context.reshape(group_rows, head_width)
-        token_context = lax.all_to_all(context, "head", split_axis=0, concat_axis=1, tiled=True)
+        mixed_arr = lax.all_to_all(
+            jnp.stack(jnp.split(context, lax.axis_size("head"), 0), axis=0), "head", 0, 0
+        )
+        token_context = jnp.concatenate(mixed_arr, 1)
         attended = (
             jnp.dot(token_context, out_weight[layer_index], preferred_element_type=jnp.float32)
             + out_bias[layer_index]

time: 1420 us -> 1420 us (level)
    all_to_all x4 -> x0, local copies, waits for them, and re-layouts: 23.6 us -> none  [on_device(): lax.all_to_all(context, 'head', split_axis=0, concat_axis=1, tiled=True)]
    split x0 -> x10, local copies, waits for them, and re-layouts: none -> 17.6 us  [on_device(): jnp.split(context, lax.axis_size('head'), 0)]
    unnamed x195 -> x209, local copies, waits for them, and re-layouts: 57.6 us -> 59 us
where the time goes in v1:
time: 1420 us; the launch traced here: 1410 us
  waiting for transfers between devices  609 us (43%)
  matrix products  477 us (34%)
  local copies, waits for them, and re-layouts  184 us (13%)
  other arithmetic  107 us (8%)
  starting transfers between devices  17 us (1%)
  between operations  15.7 us (1%)
    psum x1, waiting for transfers between devices, on_device(): small_sum, shift_sum = lax.psum((small_stack, shift_stack), ('dp', 'head'))  123 us
    reduce_scatter x1, waiting for transfers between devices, on_device(): lax.psum_scatter(ffn_stack.astype(jnp.bfloat16), 'dp', scatter_dimension=...  112 us
    reduce_scatter x2, waiting for transfers between devices, on_device(): lax.psum_scatter(jnp.einsum('rce,cde->rd', grad_proj, layer_weights, pref...  100 us
    all_gather x2, waiting for transfers between devices, on_device(): lax.all_gather(hidden_state.astype(jnp.bfloat16), 'head', axis=0, tiled=T...  92.3 us
    unnamed x12, waiting for transfers between devices  89.2 us
    dot_general x2, matrix products, on_device(): jnp.dot(ffn_rows, up_part, preferred_element_type=jnp.float32) + up_shift  78.1 us
    unnamed x209, local copies, waits for them, and re-layouts  59 us
    dot_general x32, matrix products, slot_scores(): jnp.einsum('qhd,khd->hqk', queries, keys_in, preferred_element_type=jnp.f...  55.3 us
  transfers between devices with their start and end apart: 14, of which 13 were waited for; matrix products, arithmetic and copies ran while one was open for 21% of the time, Pallas kernels for 0%

profile of v1, /device:TPU:0, one launch (start us, length us, event | category | flops | bytes accessed | tf_op | source)
XLA Modules:
  0.0 1410.0 jit_solution(3114345303787107632)
XLA Ops:
  12.9 45.8 %all-gather.3.cloned.1.call-done = bf16[4096,768]{1,0:T(8,128)(2,1)} async-done(((bf16[1024,768]{1,0:T(8,128)(2,1)}), bf16[4096,768]{1,0:T(8,128)(2,1)}) %all-gather.3.cloned.1.call-update) | async-done | bytes 6291472 | tf_op jit(solution)/shard_map/all_gather | solution.py:110
  73.9 35.5 %while.52 = (s32[]{:T(128)}, bf16[8,512,3,64]{1,3,2,0:T(8,128)(2,1)}, f32[8,3,512]{2,1,0:T(4,128)S(1)}, bf16[8,512,3,64]{1,3,2,0:T(8,128)(2,1)}, s32[8,512]{1,0:...) while((s32[]{:T(128)}, ...), condition=%wide.region_5.6_spmd, body=%wide.region_2.5_spmd.sunk | while | flops 211122688 | bytes 11335773 | solution.py:123
  133.2 15.2 %all-to-all-done = bf16[4,1024,192]{1,2,0:T(8,128)(2,1)S(1)} async-done(((bf16[4,1024,192]{1,2,0:T(8,128)(2,1)}), bf16[4,1024,192]{1,2,0:T(8,128)(2,1)S(1)}, u32[]{:S(2)}, u32[]{:S(2)}) %all-to-all-start) | async-done | bytes 1572896 | tf_op jit(solution)/shard_map/all_to_all | solution.py:127
  153.0 39.1 %multiply_convert_fusion.3 = (bf16[1024,3072]{1,0:T(8,128)(2,1)}, f32[1024,3072]{1,0:T(8,128)}, f32[1024,3072]{1,0:T(8,128)}) fusion(f32[3072]{0:T(1024)S(1)} %bitcast.502, bf16[2,768,3072]{2,1,0:T(8,128)(2,1)} %param.31, f32[1024,768]{0,1:T(8,128)S(1)} %get-tuple-element.486, f32[768]{0:T(1024)S(1)} %get-tuple-element.347, ...), kind=kOutput, calls=%fused_computation.148 | convolution fusion | flops 5043388416 | bytes 39348224 | tf_op jit(solution)/shard_map/dot_general | solution.py:142
  203.1 46.5 %all-gather.5.cloned.1.call-done = bf16[4096,768]{0,1:T(8,128)(2,1)} async-done(((bf16[1024,768]{0,1:T(8,128)(2,1)}), bf16[4096,768]{0,1:T(8,128)(2,1)}) %all-gather.5.cloned.1.call-update) | async-done | bytes 6291472 | tf_op jit(solution)/shard_map/all_gather | solution.py:110
  267.4 43.5 %while.53 = (s32[]{:T(128)}, bf16[8,512,3,64]{1,3,2,0:T(8,128)(2,1)}, f32[8,3,512]{2,1,0:T(4,128)S(1)}, bf16[8,512,3,64]{1,3,2,0:T(8,128)(2,1)}, s32[8,512]{1,0:...) while((s32[]{:T(128)}, ...), condition=%wide.region_13.14_spmd, body=%wide.region_10.13_spmd.sunk | while | flops 211122688 | bytes 11335773 | solution.py:123
  337.4 17.6 %all-to-all-done.1 = bf16[4,1024,192]{1,2,0:T(8,128)(2,1)} async-done(((bf16[4,1024,192]{1,2,0:T(8,128)(2,1)}), bf16[4,1024,192]{1,2,0:T(8,128)(2,1)}, u32[]{:S(2)}, u32[]{:S(2)}) %all-to-all-start.1) | async-done | bytes 1572896 | tf_op jit(solution)/shard_map/all_to_all | solution.py:127
  359.7 39.0 %multiply_convert_fusion.2 = (bf16[1024,3072]{1,0:T(8,128)(2,1)}, f32[1024,3072]{1,0:T(8,128)}, f32[1024,3072]{1,0:T(8,128)}) fusion(f32[3072]{0:T(1024)S(1)} %bitcast.505, bf16[2,768,3072]{2,1,0:T(8,128)(2,1)} %param.31, f32[1024,768]{0,1:T(8,128)S(1)} %get-tuple-element.491, f32[768]{0:T(1024)S(1)} %copy-done.80, f32[768]{0:T(1024)S(1)} %copy-done.57, ...), kind=kOutput, calls=%fused_computation.135 | convolution fusion | flops 5043388416 | bytes 39348224 | tf_op jit(solution)/shard_map/dot_general | solution.py:142
  414.9 18.2 %convert_reduce_fusion = (f32[3072]{0:T(1024)}, bf16[1024,3072]{1,0:T(8,128)(2,1)}) fusion(f32[1024,3072]{1,0:T(8,128)} %get-tuple-element.435, bf16[1024,768]{0,1:T(8,128)(2,1)S(1)} %get-tuple-element.425, bf16[2,3072,768]{2,1,0:T(8,128)(2,1)} %param.33, f32[1024,3072]{1,0:T(8,128)} %get-tuple-element.492, f32[3072]{0:T(1024)S(1)} %bitcast.506), kind=kOutput, calls=%fused_computation.131 | convolution fusion | flops 4885312512 | bytes 37773312 | tf_op jit(solution)/shard_map/rd,fd->rf/dot_general | solution.py:188
  433.1 11.7 multiply_reduce_fusion.2
  455.2 20.0 %all-to-all-done.2 = bf16[1024,4,192]{0,2,1:T(8,128)(2,1)S(1)} async-done(((bf16[1024,4,192]{0,2,1:T(8,128)(2,1)}), bf16[1024,4,192]{0,2,1:T(8,128)(2,1)S(1)}, u32[]{:S(2)}, u32[]{:S(2)}) %all-to-all-start.2) | async-done | bytes 1572896 | tf_op jit(solution)/shard_map/all_to_all | solution.py:211
  483.3 88.3 %while.54 = (s32[]{:T(128)}, bf16[8,512,3,64]{1,3,2,0:T(8,128)(2,1)S(1)}, bf16[8,512,3,64]{1,3,2,0:T(8,128)(2,1)}, bf16[8,512,3,64]{1,3,2,0:T(8,128)(2,1)}, bf16...) while((s32[]{:T(128)}, ...), condition=%wide.region_24.25_spmd, body=%wide.region_22.24_spmd.sunk | while | flops 511146496 | bytes 26125428 | solution.py:213
  602.7 11.8 fusion.140
  614.5 41.3 %reduce-scatter.12.cloned.1.call-done = bf16[1024,768]{0,1:T(8,128)(2,1)} async-done(((bf16[4096,768]{0,1:T(8,128)(2,1)}), bf16[1024,768]{0,1:T(8,128)(2,1)}) %reduce-scatter.12.cloned.1.call-update) | async-done | bytes 1572880 | tf_op jit(solution)/shard_map/reduce_scatter | solution.py:236
  663.0 18.5 %convert_reduce_fusion.1 = (f32[3072]{0:T(1024)S(1)}, bf16[1024,3072]{1,0:T(8,128)(2,1)}) fusion(f32[1024,3072]{1,0:T(8,128)} %get-tuple-element.437, bf16[1024,768]{0,1:T(8,128)(2,1)} %get-tuple-element.421, bf16[2,3072,768]{2,1,0:T(8,128)(2,1)} %param.33, f32[1024,3072]{1,0:T(8,128)} %get-tuple-element.487, f32[3072]{0:T(1024)S(1)} %bitcast.503), kind=kOutput, calls=%fused_computation.132 | convolution fusion | flops 4885312512 | bytes 37773312 | tf_op jit(solution)/shard_map/rd,fd->rf/dot_general | solution.py:188
  742.1 16.7 %pad_maximum_fusion = bf16[2,2,768,3072]{3,2,1,0:T(8,128)(2,1)} fusion(bf16[1,2,768,3072]{3,2,1,0:T(8,128)(2,1)} %maximum_bitcast_fusion.1, bf16[1,2,768,3072]{3,2,1,0:T(8,128)(2,1)} %maximum_bitcast_fusion), kind=kLoop, calls=%fused_computation.126 | loop fusion | flops 9437184 | bytes 37748736 | tf_op jit(solution)/shard_map/stack | solution.py:267
  781.8 10.0 all-to-all-done.3
  806.2 102.3 %while.55 = (s32[]{:T(128)}, bf16[8,512,3,64]{1,3,2,0:T(8,128)(2,1)}, bf16[8,512,3,64]{1,3,2,0:T(8,128)(2,1)}, bf16[8,512,3,64]{1,3,2,0:T(8,128)(2,1)}, bf16[8,5...) while((s32[]{:T(128)}, ...), condition=%wide.region_32.33_spmd, body=%wide.region_30.32_spmd.sunk | while | flops 511146496 | bytes 26125428 | solution.py:213
  971.3 111.5 %reduce-scatter.18.cloned.1.call-done = bf16[2,2,96,3072]{3,2,1,0:T(8,128)(2,1)} async-done(((bf16[2,2,768,3072]{3,2,1,0:T(8,128)(2,1)}), bf16[2,2,96,3072]{3,2,1,0:T(8,128)(2,1)}) %reduce-scatter.18.cloned.1.call-update) | async-done | bytes 2359312 | tf_op jit(solution)/shard_map/reduce_scatter | solution.py:273
  1085.4 122.8 %all-reduce.3.cloned.1.call-done = (f32[2,8,768]{2,0,1:T(2,128)}, f32[2,3072]{1,0:T(2,128)}) async-done(((f32[2,8,768]{2,0,1:T(2,128)}, f32[2,3072]{1,0:T(2,128)}), (f32[2,8,768]{2,0,1:T(2,128)}, f32[2,3072]{1,0:T(2,128)})) %all-reduce.3.cloned.1.call-update) | async-done | bytes 73744 | tf_op jit(solution)/shard_map/psum | solution.py:291
  1210.9 69.8 %reduce-scatter.22.cloned.1.call-done = bf16[96,1152]{1,0:T(8,128)(2,1)} async-done(((bf16[768,1152]{1,0:T(8,128)(2,1)}), bf16[96,1152]{1,0:T(8,128)(2,1)}) %reduce-scatter.22.cloned.1.call-update) | async-done | bytes 221200
  1285.0 18.6 %reduce-scatter.24.cloned.1.call-done = bf16[192,192]{1,0:T(8,128)(2,1)} async-done(((bf16[768,192]{1,0:T(8,128)(2,1)}), bf16[192,192]{1,0:T(8,128)(2,1)}) %reduce-scatter.24.cloned.1.call-update) | async-done | bytes 73744
  1305.3 59.1 %reduce-scatter.14.cloned.1.call-done = bf16[1024,768]{0,1:T(8,128)(2,1)} async-done(((bf16[4096,768]{0,1:T(8,128)(2,1)}), bf16[1024,768]{0,1:T(8,128)(2,1)}) %reduce-scatter.14.cloned.1.call-update) | async-done | bytes 1572880 | tf_op jit(solution)/shard_map/reduce_scatter | solution.py:236
  1370.2 29.9 %reduce-scatter.20.cloned.1.call-done = bf16[2,2,96,768]{3,2,1,0:T(8,128)(2,1)} async-done(((bf16[2,2,96,3072]{3,2,1,0:T(8,128)(2,1)}), bf16[2,2,96,768]{3,2,1,0:T(8,128)(2,1)}) %reduce-scatter.20.cloned.1.call-update) | async-done | bytes 589840 | tf_op jit(solution)/shard_map/reduce_scatter | solution.py:284
  (627 shorter events, 630.0 us)
Async XLA Ops:
  7.2 51.5 %all-gather.3.cloned.1.call-start = ((), (), s32[]{:S(2)}) async-start(), calls=%async_computation.11 | async-start | bytes 7864320 | tf_op jit(solution)/shard_map/all_gather | solution.py:110
  124.7 23.8 %all-to-all-start = ((bf16[4,1024,192]{1,2,0:T(8,128)(2,1)}), bf16[4,1024,192]{1,2,0:T(8,128)(2,1)S(1)}, u32[]{:S(2)}, u32[]{:S(2)}) async-start(bf16[4,1024,192]{1,2,0:T(8,128)(2,1)} %pad_maximum_fusion.3), calls=%async_computation | async-start | bytes 3145728 | tf_op jit(solution)/shard_map/all_to_all | solution.py:127
  128.4 121.2 %all-gather.5.cloned.1.call-start = ((), (), s32[]{:S(2)}) async-start(), calls=%async_computation.12 | async-start | bytes 7864320 | tf_op jit(solution)/shard_map/all_gather | solution.py:110
  132.0 60.2 %copy-start.55 = (f32[768]{0:T(1024)}, f32[768]{0:T(1024)S(1)}, u32[]{:S(2)}) copy-start(f32[768]{0:T(1024)S(1)} %get-tuple-element.503) | copy-start | bytes 9220
  132.0 60.2 %copy-start.78 = (f32[768]{0:T(1024)}, f32[768]{0:T(1024)S(1)}, u32[]{:S(2)}) copy-start(f32[768]{0:T(1024)S(1)} %get-tuple-element.347) | copy-start | bytes 9220
  132.6 68.7 %copy-start.38 = (f32[768]{0:T(1024)}, f32[768]{0:T(1024)S(1)}, u32[]{:S(2)}) copy-start(f32[768]{0:T(1024)S(1)} %get-tuple-element.505) | copy-start | bytes 9220
  132.6 68.7 %copy-start.59 = (f32[768]{0:T(1024)}, f32[768]{0:T(1024)S(1)}, u32[]{:S(2)}) copy-start(f32[768]{0:T(1024)S(1)} %get-tuple-element.341) | copy-start | bytes 9220
  200.9 154.1 %copy-start = (f32[1024,768]{0,1:T(8,128)}, f32[1024,768]{0,1:T(8,128)S(1)}, u32[]{:S(2)}) copy-start(f32[1024,768]{0,1:T(8,128)S(1)} %get-tuple-element.489) | copy-start | bytes 9437188
  330.5 24.5 %all-to-all-start.1 = ((bf16[4,1024,192]{1,2,0:T(8,128)(2,1)}), bf16[4,1024,192]{1,2,0:T(8,128)(2,1)}, u32[]{:S(2)}, u32[]{:S(2)}) async-start(bf16[4,1024,192]{1,2,0:T(8,128)(2,1)} %pad_maximum_fusion.4), calls=%async_computation.1 | async-start | bytes 3145728 | tf_op jit(solution)/shard_map/all_to_all | solution.py:127
  451.6 23.6 %all-to-all-start.2 = ((bf16[1024,4,192]{0,2,1:T(8,128)(2,1)}), bf16[1024,4,192]{0,2,1:T(8,128)(2,1)S(1)}, u32[]{:S(2)}, u32[]{:S(2)}) async-start(bf16[1024,4,192]{0,2,1:T(8,128)(2,1)} %bitcast.68), calls=%async_computation.2 | async-start | bytes 3145728 | tf_op jit(solution)/shard_map/all_to_all | solution.py:211
  455.2 200.6 %reduce-scatter.12.cloned.1.call-start = ((), (), s32[]{:S(2)}) async-start(), calls=%async_computation.13 | async-start | bytes 7864320 | tf_op jit(solution)/shard_map/reduce_scatter | solution.py:236
  597.3 362.0 %reduce-scatter.16.cloned.1.call-start = ((), (), s32[]{:S(2)}) async-start(), calls=%async_computation.15 | async-start | bytes 2654208 | tf_op jit(solution)/shard_map/reduce_scatter | solution.py:276
  602.7 53.1 %copy-start.1 = (f32[1024,768]{0,1:T(8,128)S(1)}, f32[1024,768]{0,1:T(8,128)}, u32[]{:S(2)}) copy-start(f32[1024,768]{0,1:T(8,128)} %copy-done) | copy-start | bytes 9437188
  602.7 53.1 %copy-start.37 = (f32[1024]{0:T(1024)S(1)}, f32[1024]{0:T(1024)}, u32[]{:S(2)}) copy-start(f32[1024]{0:T(1024)} %copy-done.35) | copy-start | bytes 12292
  602.7 53.1 %copy-start.40 = (f32[768]{0:T(1024)S(1)}, f32[768]{0:T(1024)}, u32[]{:S(2)}) copy-start(f32[768]{0:T(1024)} %copy-done.38) | copy-start | bytes 9220
  602.7 53.1 %copy-start.43 = (f32[1024]{0:T(1024)S(1)}, f32[1024]{0:T(1024)}, u32[]{:S(2)}) copy-start(f32[1024]{0:T(1024)} %copy-done.41) | copy-start | bytes 12292
  614.5 45.2 %copy-start.50 = (f32[1024]{0:T(1024)S(1)}, f32[1024]{0:T(1024)}, u32[]{:S(2)}) copy-start(f32[1024]{0:T(1024)} %copy-done.49) | copy-start | bytes 12292
  697.1 385.8 %reduce-scatter.18.cloned.1.call-start = ((), (), s32[]{:S(2)}) async-start(), calls=%async_computation.16 | async-start | bytes 21233664 | tf_op jit(solution)/shard_map/reduce_scatter | solution.py:273
  767.3 24.5 %all-to-all-start.3 = ((bf16[1024,4,192]{0,2,1:T(8,128)(2,1)}), bf16[1024,4,192]{0,2,1:T(8,128)(2,1)}, u32[]{:S(2)}, u32[]{:S(2)}) async-start(bf16[1024,4,192]{0,2,1:T(8,128)(2,1)} %bitcast.491), calls=%async_computation.4 | async-start | bytes 3145728 | tf_op jit(solution)/shard_map/all_to_all | solution.py:211
  771.7 436.6 %all-reduce.3.cloned.1.call-start = ((), (), s32[]{:S(2)}) async-start(), calls=%async_computation.20 | async-start | bytes 147456 | tf_op jit(solution)/shard_map/psum | solution.py:291
  936.6 344.1 %reduce-scatter.22.cloned.1.call-start = ((), (), s32[]{:S(2)}) async-start(), calls=%async_computation.18 | async-start | bytes 1990656
  959.2 344.3 %reduce-scatter.24.cloned.1.call-start = ((), (), s32[]{:S(2)}) async-start(), calls=%async_computation.19 | async-start | bytes 491520
  961.5 402.9 %reduce-scatter.14.cloned.1.call-start = ((), (), s32[]{:S(2)}) async-start(), calls=%async_computation.14 | async-start | bytes 7864320 | tf_op jit(solution)/shard_map/reduce_scatter | solution.py:236
  971.3 428.8 %reduce-scatter.20.cloned.1.call-start = ((), (), s32[]{:S(2)}) async-start(), calls=%async_computation.17 | async-start | bytes 2949120 | tf_op jit(solution)/shard_map/reduce_scatter | solution.py:284
  (82 other events, 1061.3 us)
Sparse Core Ops, SparseCore 0:
  9.6 49.0 all-gather.2
  203.2 46.3 all-gather.4
  597.4 58.3 reduce-scatter.11
  697.2 69.0 reduce-scatter.15
  770.4 312.3 reduce-scatter.17
  1090.4 117.7 all-reduce.2
  1212.1 68.5 reduce-scatter.21
  1283.8 19.7 reduce-scatter.23
  1306.1 58.3 reduce-scatter.13
  1367.0 33.0 reduce-scatter.19
